TPU v7x, 32 devices: a whole 2x2x4 slice. The times are simulated.
32 devices in a mesh: grp: 2 (over y), row: 4 (over x, core), col: 4 (over z).
Axes of the slice: x: 2, y: 2, z: 4, core: 2. Of those that a mesh axis runs over, the one named last changes fastest.
Arguments:
- perturbation: bfloat16 [4, 12000, 12000], P('grp', 'row', 'col'), parts along dimension 0, may hold values from -96 to 96
- occ_coeffs: bfloat16 [12000, 2000], P('row', 'col'), may hold values from -0.0546875 to 0.0546875
- vir_coeffs: bfloat16 [12000, 512], P('col', 'row'), may hold values from -0.0546875 to 0.0546875
- occ_energies: float32 [2000], replicated, may hold values from -1 to -0.1
- vir_energies: float32 [512], replicated, may hold values from 0.1 to 1.5
Outputs:
- density_response: bfloat16 [4, 12000, 12000], P('grp', 'row', 'col'), parts along dimension 0
There are 2 independent parts, one for each index of `grp`. A program takes and returns all parts, laid end to end along the dimension named above; an argument that names none is the same for every part. Nothing has to cross between parts.
All inputs are finite; a program needn't handle non-finite values.
Results may differ from a plain program's by a relative error of at most 0.0098.
Values may be sent and summed in bfloat16 or wider, within the bound.
A program may use at most 192 MiB of HBM per device.

v0:
```python
import jax
import jax.numpy as jnp
from jax import lax
from jax.sharding import PartitionSpec as P

BF16 = jnp.bfloat16
F32 = jnp.float32


def per_device(perturbation, occ_coeffs, vir_coeffs, occ_energies, vir_energies):
    vir_rows = lax.all_gather(vir_coeffs, "row", axis=1, tiled=True)
    occ_parts = lax.all_gather(occ_coeffs, "col")
    cols, _, width = occ_parts.shape
    image = jnp.einsum("pij,jv->piv", perturbation, vir_rows, preferred_element_type=F32).astype(
        BF16
    )
    part = jnp.einsum("cio,piv->pcov", occ_parts, image, preferred_element_type=F32).astype(BF16)
    coupling = lax.psum(part, ("row", "col"))
    gaps = occ_energies.reshape(cols, width)[:, :, None] - vir_energies[None, None, :]
    response = (coupling.astype(F32) / gaps[None]).astype(BF16)
    mixed = jnp.einsum("cio,pcov->piv", occ_parts, response, preferred_element_type=F32).astype(
        BF16
    )
    return jnp.einsum("piv,jv->pij", mixed, vir_rows, preferred_element_type=F32).astype(BF16)


def solution(mesh):
    placed = (P("grp", "row", "col"), P("row", "col"), P("col", "row"), P(), P())
    return jax.shard_map(
        per_device, mesh=mesh, in_specs=placed, out_specs=P("grp", "row", "col"), check_vma=False
    )
```

profile of v0, /device:TPU:0, one launch (start us, length us, event | category | flops | bytes accessed | tf_op | source)
XLA Modules:
  0.0 448.0 jit_solution(10581064769501468559)
XLA Ops:
  6.5 0.0 all-gather.4.cloned.1.call-start
  6.5 0.7 all-gather.4.cloned.1.call-update
  7.3 0.0 all-gather.6.cloned.1.call-start
  7.3 0.7 all-gather.6.cloned.1.call-update
  8.0 0.0 all-reduce.2.cloned.1.call-start
  8.1 32.1 %all-gather.4.cloned.1.call-done = bf16[3000,512]{1,0:T(8,128)(2,1)} async-done(((bf16[3000,128]{1,0:T(8,128)(2,1)}), bf16[3000,512]{1,0:T(8,128)(2,1)}) %all-gather.4.cloned.1.call-update) | async-done | bytes 3072016 | tf_op jit(solution)/shard_map/all_gather | solution.py:11
  40.1 25.8 %fusion.45 = bf16[2,3000,512,1]{2,1,3,0:T(8,128)(2,1)} fusion(bf16[2,3000,3000]{2,1,0:T(8,128)(2,1)} %param.5, bf16[3000,512]{1,0:T(8,128)(2,1)} %all-gather.4.cloned.1.call-done), kind=kOutput, calls=%fused_computation.5.clone.clone.clone.1 | convolution fusion | flops 18435072000 | bytes 45216000 | tf_op jit(solution)/shard_map/pij,jv->piv/dot_general | solution.py:14
  66.0 189.1 %all-gather.6.cloned.1.call-done = bf16[12000,500]{1,0:T(8,128)(2,1)} async-done(((bf16[3000,500]{1,0:T(8,128)(2,1)}), bf16[12000,500]{1,0:T(8,128)(2,1)}) %all-gather.6.cloned.1.call-update) | async-done | bytes 12000016 | tf_op jit(solution)/shard_map/all_gather | solution.py:12
  255.1 19.1 %fusion.17 = bf16[2,512,4,500]{1,3,2,0:T(8,128)(2,1)} fusion(bf16[4,3000,500,1]{2,1,0,3:T(8,128)(2,1)} %bitcast.58, bf16[2,3000,512,1]{2,1,3,0:T(8,128)(2,1)} %fusion.45), kind=kOutput, calls=%fused_computation.12 | convolution fusion | flops 12290048000 | bytes 22240000 | tf_op jit(solution)/shard_map/cio,piv->pcov/dot_general | solution.py:17
  274.2 0.0 copy-start
  274.2 0.0 copy-start.1
  274.2 7.8 %copy.10 = bf16[2,512,4,500]{3,2,1,0:T(4,128)(2,1)} copy(bf16[2,512,4,500]{1,3,2,0:T(8,128)(2,1)} %fusion.17) | data formatting | bytes 8192000
  282.0 0.0 all-reduce.2.cloned.1.call-update
  282.0 0.0 copy-done
  282.1 0.1 sub.19
  282.1 0.0 copy-done.1
  282.1 2.8 broadcast_subtract_fusion
  285.0 106.6 %all-reduce.2.cloned.1.call-done = bf16[2,4,500,512]{2,1,3,0:T(4,128)(2,1)} async-done(((bf16[2,4,500,512]{2,1,3,0:T(4,128)(2,1)}), bf16[2,4,500,512]{2,1,3,0:T(4,128)(2,1)}) %all-reduce.2.cloned.1.call-update) | async-done | bytes 4096016 | tf_op jit(solution)/shard_map/psum | solution.py:18
  391.5 5.5 %fusion = bf16[2,4,500,512]{2,1,3,0:T(4,128)(2,1)S(1)} fusion(bf16[2,4,500,512]{2,1,3,0:T(4,128)(2,1)} %all-reduce.2.cloned.1.call-done, f32[4,500,512]{1,0,2:T(4,128)} %broadcast_subtract_fusion), kind=kLoop, calls=%fused_computation.3 | loop fusion | flops 6144000 | bytes 12288000 | tf_op jit(solution)/shard_map/convert_element_type | solution.py:20
  397.1 16.8 %fusion.41 = bf16[2,3000,512]{2,1,0:T(8,128)(2,1)} fusion(bf16[4,3000,500,1]{2,1,0,3:T(8,128)(2,1)} %bitcast.59, bf16[2,4,500,512]{2,1,3,0:T(4,128)(2,1)S(1)} %fusion), kind=kOutput, calls=%fused_computation.6.clone.1 | convolution fusion | flops 12291072000 | bytes 22240000 | tf_op jit(solution)/shard_map/cio,pcov->piv/dot_general | solution.py:21
  413.9 27.6 %convolution_convert_fusion = bf16[2,3000,3000]{2,1,0:T(8,128)(2,1)} fusion(bf16[3000,512]{1,0:T(8,128)(2,1)} %all-gather.4.cloned.1.call-done, bf16[2,3000,512]{2,1,0:T(8,128)(2,1)} %fusion.41), kind=kOutput, calls=%fused_computation | convolution fusion | flops 18449999872 | bytes 45216000 | tf_op jit(solution)/shard_map/piv,jv->pij/dot_general | solution.py:24
Async XLA Ops:
  6.5 33.6 %all-gather.4.cloned.1.call-start = ((), (), s32[]{:S(2)}) async-start(), calls=%async_computation | async-start | bytes 3840000 | tf_op jit(solution)/shard_map/all_gather | solution.py:11
  7.3 247.8 %all-gather.6.cloned.1.call-start = ((), (), s32[]{:S(2)}) async-start(), calls=%async_computation.2 | async-start | bytes 15360000 | tf_op jit(solution)/shard_map/all_gather | solution.py:12
  8.0 383.5 %all-reduce.2.cloned.1.call-start = ((), (), s32[]{:S(2)}) async-start(), calls=%async_computation.1 | async-start | bytes 8388608 | tf_op jit(solution)/shard_map/psum | solution.py:18
  274.2 7.9 %copy-start = (f32[2000]{0:T(1024)S(1)}, f32[2000]{0:T(1024)}, u32[]{:S(2)}) copy-start(f32[2000]{0:T(1024)} %param.8) | copy-start | bytes 24004
  274.2 8.0 %copy-start.1 = (f32[512]{0:T(512)S(1)}, f32[512]{0:T(512)}, u32[]{:S(2)}) copy-start(f32[512]{0:T(512)} %param.9) | copy-start | bytes 6148
Sparse Core Ops, SparseCore 0:
  8.9 31.1 all-gather.3
  41.7 213.3 all-gather.5
  282.2 109.3 all-reduce.1
where the time goes:
time: 448 us
  waiting for transfers between devices  329 us (73%)
  matrix products  89.4 us (20%)
  between operations  13.1 us (3%)
  other arithmetic  8.38 us (2%)
  local copies, waits for them, and re-layouts  7.93 us (2%)
    all_gather x1, waiting for transfers between devices, per_device(): occ_parts = lax.all_gather(occ_coeffs, 'col')  189 us
    psum x1, waiting for transfers between devices, per_device(): coupling = lax.psum(part, ('row', 'col'))  107 us
    all_gather x1, waiting for transfers between devices, per_device(): vir_rows = lax.all_gather(vir_coeffs, 'row', axis=1, tiled=True)  32.1 us
    dot_general x1, matrix products, per_device(): jnp.einsum('piv,jv->pij', mixed, vir_rows, preferred_element_type=F32)  27.6 us
    dot_general x1, matrix products, per_device(): jnp.einsum('pij,jv->piv', perturbation, vir_rows, preferred_element_type=...  25.8 us
    dot_general x1, matrix products, per_device(): jnp.einsum('cio,piv->pcov', occ_parts, image, preferred_element_type=F32)  19.1 us
    dot_general x1, matrix products, per_device(): jnp.einsum('cio,pcov->piv', occ_parts, response, preferred_element_type=F32)  16.8 us
  transfers between devices with their start and end apart: 3, of which 3 were waited for; matrix products, arithmetic and copies ran while one was open for 6% of the time, Pallas kernels for 0%

commit v1 on v0

--- a/solution.py
+++ b/solution.py
@@ -15,7 +15,7 @@
         BF16
     )
     part = jnp.einsum("cio,piv->pcov", occ_parts, image, preferred_element_type=F32).astype(BF16)
-    coupling = lax.psum(part, ("row", "col"))
+    coupling = lax.psum(lax.psum(part, "col"), "row")
     gaps = occ_energies.reshape(cols, width)[:, :, None] - vir_energies[None, None, :]
     response = (coupling.astype(F32) / gaps[None]).astype(BF16)
     mixed = jnp.einsum("cio,pcov->piv", occ_parts, response, preferred_element_type=F32).astype(

time: 448 us -> 579 us (1.29)
  waiting for transfers between devices: 329 us -> 459 us
    psum x1 -> x2, waiting for transfers between devices: 107 us -> 237 us  [per_device(): coupling = lax.psum(lax.psum(part, 'col'), 'row')]
  transfers between devices with their start and end apart: 3 -> 4, of which waited for: 3 -> 4; matrix products, arithmetic and copies ran while one was open for 6% -> 5% of each run, Pallas kernels for 0% -> 0%
where the time goes in v1:
time: 579 us
  waiting for transfers between devices  459 us (79%)
  matrix products  89.4 us (15%)
  between operations  13.1 us (2%)
  other arithmetic  8.39 us (1%)
  local copies, waits for them, and re-layouts  7.9 us (1%)
    psum x2, waiting for transfers between devices, per_device(): coupling = lax.psum(lax.psum(part, 'col'), 'row')  237 us
    all_gather x1, waiting for transfers between devices, per_device(): occ_parts = lax.all_gather(occ_coeffs, 'col')  189 us
    all_gather x1, waiting for transfers between devices, per_device(): vir_rows = lax.all_gather(vir_coeffs, 'row', axis=1, tiled=True)  32.1 us
    dot_general x1, matrix products, per_device(): jnp.einsum('piv,jv->pij', mixed, vir_rows, preferred_element_type=F32)  27.6 us
    dot_general x1, matrix products, per_device(): jnp.einsum('pij,jv->piv', perturbation, vir_rows, preferred_element_type=...  25.8 us
    dot_general x1, matrix products, per_device(): jnp.einsum('cio,piv->pcov', occ_parts, image, preferred_element_type=F32)  19.1 us
    dot_general x1, matrix products, per_device(): jnp.einsum('cio,pcov->piv', occ_parts, response, preferred_element_type=F32)  16.8 us
  transfers between devices with their start and end apart: 4, of which 4 were waited for; matrix products, arithmetic and copies ran while one was open for 5% of the time, Pallas kernels for 0%

profile of v1, /device:TPU:0, one launch (start us, length us, event | category | flops | bytes accessed | tf_op | source)
XLA Modules:
  0.0 578.6 jit_solution(4163890639878657360)
XLA Ops:
  6.5 0.0 all-gather.4.cloned.1.call-start
  6.5 0.7 all-gather.4.cloned.1.call-update
  7.3 0.0 all-gather.6.cloned.1.call-start
  7.3 0.7 all-gather.6.cloned.1.call-update
  8.0 0.0 all-reduce.3.cloned.1.call-start
  8.1 32.1 %all-gather.4.cloned.1.call-done = bf16[3000,512]{1,0:T(8,128)(2,1)} async-done(((bf16[3000,128]{1,0:T(8,128)(2,1)}), bf16[3000,512]{1,0:T(8,128)(2,1)}) %all-gather.4.cloned.1.call-update) | async-done | bytes 3072016 | tf_op jit(solution)/shard_map/all_gather | solution.py:11
  40.1 25.8 %fusion.45 = bf16[2,3000,512,1]{2,1,3,0:T(8,128)(2,1)} fusion(bf16[2,3000,3000]{2,1,0:T(8,128)(2,1)} %param.5, bf16[3000,512]{1,0:T(8,128)(2,1)} %all-gather.4.cloned.1.call-done), kind=kOutput, calls=%fused_computation.5.clone.clone.clone.1 | convolution fusion | flops 18435072000 | bytes 45216000 | tf_op jit(solution)/shard_map/pij,jv->piv/dot_general | solution.py:14
  66.0 189.1 %all-gather.6.cloned.1.call-done = bf16[12000,500]{1,0:T(8,128)(2,1)} async-done(((bf16[3000,500]{1,0:T(8,128)(2,1)}), bf16[12000,500]{1,0:T(8,128)(2,1)}) %all-gather.6.cloned.1.call-update) | async-done | bytes 12000016 | tf_op jit(solution)/shard_map/all_gather | solution.py:12
  255.1 19.1 %fusion.17 = bf16[2,512,4,500]{1,3,2,0:T(8,128)(2,1)} fusion(bf16[4,3000,500,1]{2,1,0,3:T(8,128)(2,1)} %bitcast.58, bf16[2,3000,512,1]{2,1,3,0:T(8,128)(2,1)} %fusion.45), kind=kOutput, calls=%fused_computation.12 | convolution fusion | flops 12290048000 | bytes 22240000 | tf_op jit(solution)/shard_map/cio,piv->pcov/dot_general | solution.py:17
  274.2 7.8 %copy.10 = bf16[2,512,4,500]{3,2,1,0:T(4,128)(2,1)} copy(bf16[2,512,4,500]{1,3,2,0:T(8,128)(2,1)} %fusion.17) | data formatting | bytes 8192000
  282.0 0.0 copy-start
  282.0 0.0 copy-start.1
  282.0 0.0 all-reduce.3.cloned.1.call-update
  282.0 0.2 all-reduce.5.cloned.1.call-start
  282.2 153.1 %all-reduce.3.cloned.1.call-done = bf16[2,4,500,512]{2,1,3,0:T(4,128)(2,1)} async-done(((bf16[2,4,500,512]{2,1,3,0:T(4,128)(2,1)}), bf16[2,4,500,512]{2,1,3,0:T(4,128)(2,1)}) %all-reduce.3.cloned.1.call-update) | async-done | bytes 4096016 | tf_op jit(solution)/shard_map/psum | solution.py:18
  435.3 0.0 all-reduce.5.cloned.1.call-update
  435.4 0.0 copy-done
  435.4 0.1 sub.19
  435.5 0.0 copy-done.1
  435.5 2.8 broadcast_subtract_fusion
  438.3 83.7 %all-reduce.5.cloned.1.call-done = bf16[2,4,500,512]{2,1,3,0:T(4,128)(2,1)} async-done(((bf16[2,4,500,512]{2,1,3,0:T(4,128)(2,1)}), bf16[2,4,500,512]{2,1,3,0:T(4,128)(2,1)}) %all-reduce.5.cloned.1.call-update) | async-done | bytes 4096016 | tf_op jit(solution)/shard_map/psum | solution.py:18
  522.1 5.5 fusion
  527.6 16.8 %fusion.41 = bf16[2,3000,512]{2,1,0:T(8,128)(2,1)} fusion(bf16[4,3000,500,1]{2,1,0,3:T(8,128)(2,1)} %bitcast.59, bf16[2,4,500,512]{2,1,3,0:T(4,128)(2,1)S(1)} %fusion), kind=kOutput, calls=%fused_computation.6.clone.1 | convolution fusion | flops 12291072000 | bytes 22240000 | tf_op jit(solution)/shard_map/cio,pcov->piv/dot_general | solution.py:21
  544.4 27.6 %convolution_convert_fusion = bf16[2,3000,3000]{2,1,0:T(8,128)(2,1)} fusion(bf16[3000,512]{1,0:T(8,128)(2,1)} %all-gather.4.cloned.1.call-done, bf16[2,3000,512]{2,1,0:T(8,128)(2,1)} %fusion.41), kind=kOutput, calls=%fused_computation | convolution fusion | flops 18449999872 | bytes 45216000 | tf_op jit(solution)/shard_map/piv,jv->pij/dot_general | solution.py:24
Async XLA Ops:
  6.5 33.6 %all-gather.4.cloned.1.call-start = ((), (), s32[]{:S(2)}) async-start(), calls=%async_computation | async-start | bytes 3840000 | tf_op jit(solution)/shard_map/all_gather | solution.py:11
  7.3 247.8 %all-gather.6.cloned.1.call-start = ((), (), s32[]{:S(2)}) async-start(), calls=%async_computation.3 | async-start | bytes 15360000 | tf_op jit(solution)/shard_map/all_gather | solution.py:12
  8.0 427.3 %all-reduce.3.cloned.1.call-start = ((), (), s32[]{:S(2)}) async-start(), calls=%async_computation.1 | async-start | bytes 8388608 | tf_op jit(solution)/shard_map/psum | solution.py:18
  282.0 153.4 %copy-start = (f32[2000]{0:T(1024)S(1)}, f32[2000]{0:T(1024)}, u32[]{:S(2)}) copy-start(f32[2000]{0:T(1024)} %param.8) | copy-start | bytes 24004
  282.0 153.5 %copy-start.1 = (f32[512]{0:T(512)S(1)}, f32[512]{0:T(512)}, u32[]{:S(2)}) copy-start(f32[512]{0:T(512)} %param.9) | copy-start | bytes 6148
  282.0 240.0 %all-reduce.5.cloned.1.call-start = ((), (), s32[]{:S(2)}) async-start(), calls=%async_computation.2 | async-start | bytes 8388608 | tf_op jit(solution)/shard_map/psum | solution.py:18
Sparse Core Ops, SparseCore 0:
  8.9 31.1 all-gather.3
  41.7 213.3 all-gather.5
  282.1 153.1 all-reduce.2
  437.6 84.4 all-reduce.4
